TPU v7x, 32 devices: a whole 2x2x4 slice. The times are simulated.
32 devices in a mesh: fsdp: 2 (over y), ctx: 4 (over x, core), tp: 4 (over z).
Axes of the slice: x: 2, y: 2, z: 4, core: 2. Of those that a mesh axis runs over, the one named last changes fastest.
Arguments:
- block_input: bfloat16 [4, 2048, 1024], P('fsdp', 'ctx'), may hold values from -6 to 6
- positions: int32 [3, 4, 2048], P(None, 'fsdp', 'ctx'), may hold values from 0 to 15
- w_qkv: bfloat16 [3, 1024, 1024], P(None, 'fsdp', 'tp'), may hold values from -0.1875 to 0.1875
- b_qkv: float32 [3, 1024], P(None, 'tp'), may hold values from -3 to 3
- w_proj: bfloat16 [1024, 1024], P('tp', 'fsdp'), may hold values from -1 to 1
- w_up: bfloat16 [1024, 4096], P('fsdp', 'tp'), may hold values from -0.1875 to 0.1875
- b_up: float32 [4096], P('tp'), may hold values from -3 to 3
- w_down: bfloat16 [4096, 1024], P('tp', 'fsdp'), may hold values from -0.09375 to 0.09375
- norm_gains: float32 [2, 1024], replicated, may hold values from 0.5 to 1.5
- norm_shifts: float32 [2, 1024], replicated, may hold values from -2 to 2
- out_shifts: float32 [2, 1024], replicated, may hold values from -2 to 2
- grad_out: bfloat16 [4, 2048, 1024], P('fsdp', 'ctx'), may hold values from -6 to 6
Outputs:
- block_output: bfloat16 [4, 2048, 1024], P('fsdp', 'ctx')
- grad_input: float32 [4, 2048, 1024], P('fsdp', 'ctx')
- grad_w_qkv: float32 [3, 1024, 1024], P(None, 'fsdp', 'tp')
- grad_b_qkv: float32 [3, 1024], P(None, 'tp')
- grad_w_proj: float32 [1024, 1024], P('tp', 'fsdp')
- grad_w_up: float32 [1024, 4096], P('fsdp', 'tp')
- grad_b_up: float32 [4096], P('tp')
- grad_w_down: float32 [4096, 1024], P('tp', 'fsdp')
- grad_gains: float32 [2, 1024], replicated
- grad_shifts: float32 [2, 1024], replicated
- grad_out_shifts: float32 [2, 1024], replicated
Inputs may be any that keep to these rules, and one draw needn't show every extreme that they name: `positions`: each token's time, height and width index in its clip.
All inputs are finite; a program needn't handle non-finite values.
Results may differ from a plain program's by a relative error of at most 0.02.
Values may be sent and summed in bfloat16 or wider, within the bound.
A program may use at most 128 MiB of HBM per device.

v0:
```python
from functools import partial
import jax
import jax.numpy as jnp
from jax import lax
from jax.sharding import PartitionSpec as P

HD = 64
LEN = 2048
ROT = 20
QBLK = 512
EPSILON = 1e-06


def layer_norm(values, gain_vec, shift_vec):
    center = values - jnp.mean(values, axis=-1, keepdims=True)
    spread = jnp.mean(center * center, axis=-1, keepdims=True)
    return center * lax.rsqrt(spread + EPSILON) * gain_vec + shift_vec


def rotary_tables(position_rows):
    half_rot = ROT // 2
    freqs = 10000.0 ** (-2.0 * jnp.arange(half_rot, dtype=jnp.float32) / ROT)
    angles = position_rows.astype(jnp.float32)[:, :, None] * freqs[None, None, :]
    return (jnp.cos(angles), jnp.sin(angles))


def rotary(values, cos_table, sin_table):
    half_rot = ROT // 2
    pieces = []
    for dim_index in range(3):
        offset_at = dim_index * ROT
        first_half = values[..., offset_at : offset_at + half_rot]
        second_half = values[..., offset_at + half_rot : offset_at + ROT]
        cos_part = cos_table[dim_index][:, None, :]
        sin_part = sin_table[dim_index][:, None, :]
        pieces.append(first_half * cos_part - second_half * sin_part)
        pieces.append(second_half * cos_part + first_half * sin_part)
    pieces.append(values[..., 3 * ROT :])
    return jnp.concatenate(pieces, axis=-1)


def contract_rows(left_mat, right_mat):
    return lax.dot_general(
        left_mat, right_mat, (((0,), (0,)), ((), ())), preferred_element_type=jnp.float32
    )


def contract_cols(left_mat, right_mat):
    return lax.dot_general(
        left_mat, right_mat, (((1,), (1,)), ((), ())), preferred_element_type=jnp.float32
    )


def tp_whole(partial_sum):
    return lax.psum(partial_sum.astype(jnp.bfloat16), "tp").astype(jnp.float32)


def attend_group(operands):
    queries, keys_all, values_all = operands
    score_factor = HD ** (-0.5)

    def attend_block(query_block):
        scores = (
            jnp.einsum("qe,ke->qk", query_block, keys_all, preferred_element_type=jnp.float32)
            * score_factor
        )
        largest = jnp.max(scores, axis=-1, keepdims=True)
        expon = jnp.exp(scores - largest)
        totals = jnp.sum(expon, axis=-1, keepdims=True)
        probs = expon / totals
        block_out = jnp.dot(
            probs.astype(jnp.bfloat16), values_all, preferred_element_type=jnp.float32
        )
        return (block_out.astype(jnp.bfloat16), (largest + jnp.log(totals))[:, 0])

    return lax.map(attend_block, queries.reshape(LEN // QBLK, QBLK, HD))


def backward_group(operands):
    queries, keys_all, values_all, grad_attended, log_totals = operands
    score_factor = HD ** (-0.5)

    def back_block(carry, block_items):
        grad_keys, grad_values = carry
        query_block, grad_block, log_block = block_items
        scores = (
            jnp.einsum("qe,ke->qk", query_block, keys_all, preferred_element_type=jnp.float32)
            * score_factor
        )
        probs = jnp.exp(scores - log_block[:, None])
        probs_low = probs.astype(jnp.bfloat16)
        grad_probs = jnp.einsum(
            "qe,ke->qk", grad_block, values_all, preferred_element_type=jnp.float32
        )
        inner = jnp.sum(probs * grad_probs, axis=-1, keepdims=True)
        grad_scores = (probs * (grad_probs - inner)).astype(jnp.bfloat16)
        grad_query = (
            jnp.dot(grad_scores, keys_all, preferred_element_type=jnp.float32) * score_factor
        )
        grad_keys = grad_keys + contract_rows(grad_scores, query_block) * score_factor
        grad_values = grad_values + contract_rows(probs_low, grad_block)
        return ((grad_keys, grad_values), grad_query)

    zeros_kv = jnp.zeros((LEN, HD), jnp.float32)
    block_count = LEN // QBLK
    items = (
        queries.reshape(block_count, QBLK, HD),
        grad_attended.reshape(block_count, QBLK, HD),
        log_totals,
    )
    (grad_keys, grad_values), grad_queries = lax.scan(back_block, (zeros_kv, zeros_kv), items)
    return (grad_queries.reshape(LEN, HD), grad_keys, grad_values)


def shards(
    block_input,
    positions,
    w_qkv,
    b_qkv,
    w_proj,
    w_up,
    b_up,
    w_down,
    norm_gains,
    norm_shifts,
    out_shifts,
    grad_out,
):
    clip_count, local_len, width = block_input.shape
    row_count = clip_count * local_len
    ctx_count = lax.axis_size("ctx")
    local_width = w_qkv.shape[2]
    group_heads = local_width // ctx_count // HD
    group_count = clip_count * group_heads
    inputs = block_input.reshape(row_count, width).astype(jnp.float32)
    full_qkv, full_proj, full_up, full_down = (
        lax.all_gather(w_qkv, "fsdp", axis=1, tiled=True),
        lax.all_gather(w_proj, "fsdp", axis=1, tiled=True),
        lax.all_gather(w_up, "fsdp", axis=0, tiled=True),
        lax.all_gather(w_down, "fsdp", axis=1, tiled=True),
    )
    cos_table, sin_table = rotary_tables(positions.reshape(3, row_count))
    normed_one = layer_norm(inputs, norm_gains[0], norm_shifts[0])
    normed_one_low = normed_one.astype(jnp.bfloat16)
    projected = (
        jnp.einsum("rd,cde->cre", normed_one_low, full_qkv, preferred_element_type=jnp.float32)
        + b_qkv[:, None, :]
    )
    head_shape = (row_count, local_width // HD, HD)
    queries_rot = rotary(projected[0].reshape(head_shape), cos_table, sin_table).reshape(
        row_count, local_width
    )
    keys_rot = rotary(projected[1].reshape(head_shape), cos_table, sin_table).reshape(
        row_count, local_width
    )
    token_qkv = (
        jnp.stack([queries_rot, keys_rot, projected[2]])
        .astype(jnp.bfloat16)
        .reshape(3, clip_count, local_len, local_width)
    )
    head_qkv = lax.all_to_all(token_qkv, "ctx", split_axis=3, concat_axis=2, tiled=True)
    full_len = head_qkv.shape[2]
    grouped = (
        head_qkv.reshape(3, clip_count, full_len, group_heads, HD)
        .transpose(0, 1, 3, 2, 4)
        .reshape(3, group_count, full_len, HD)
    )
    attended, log_totals = lax.map(attend_group, (grouped[0], grouped[1], grouped[2]))
    attended = (
        attended.reshape(clip_count, group_heads, full_len, HD)
        .transpose(0, 2, 1, 3)
        .reshape(clip_count, full_len, group_heads * HD)
    )
    token_attended = lax.all_to_all(
        attended, "ctx", split_axis=1, concat_axis=2, tiled=True
    ).reshape(row_count, local_width)
    attn_part = jnp.dot(token_attended, full_proj, preferred_element_type=jnp.float32)
    residual = inputs + tp_whole(attn_part) + out_shifts[0]
    normed_two_low = layer_norm(residual, norm_gains[1], norm_shifts[1]).astype(jnp.bfloat16)
    pre_act = jnp.dot(normed_two_low, full_up, preferred_element_type=jnp.float32) + b_up
    act_low = jax.nn.gelu(pre_act, approximate=False).astype(jnp.bfloat16)
    mlp_part = jnp.dot(act_low, full_down, preferred_element_type=jnp.float32)
    result = residual + tp_whole(mlp_part) + out_shifts[1]
    block_rows = result.astype(jnp.bfloat16)
    full_qkv, full_proj, full_up, full_down = (
        lax.all_gather(w_qkv, "fsdp", axis=1, tiled=True),
        lax.all_gather(w_proj, "fsdp", axis=1, tiled=True),
        lax.all_gather(w_up, "fsdp", axis=0, tiled=True),
        lax.all_gather(w_down, "fsdp", axis=1, tiled=True),
    )
    upstream = grad_out.reshape(row_count, width).astype(jnp.float32)
    upstream_low = upstream.astype(jnp.bfloat16)
    grad_down = contract_rows(act_low, upstream_low)
    grad_act = contract_cols(upstream_low, full_down)
    _, gelu_pull = jax.vjp(partial(jax.nn.gelu, approximate=False), pre_act)
    grad_pre = gelu_pull(grad_act)[0].astype(jnp.bfloat16)
    grad_b_up = jnp.sum(grad_pre.astype(jnp.float32), axis=0)
    grad_up = contract_rows(normed_two_low, grad_pre)
    back_part_two = contract_cols(grad_pre, full_up)
    grad_normed_two = tp_whole(back_part_two)
    _, norm_pull_two = jax.vjp(layer_norm, residual, norm_gains[1], norm_shifts[1])
    grad_res_norm, grad_gain_two, grad_shift_two = norm_pull_two(grad_normed_two)
    grad_residual = upstream + grad_res_norm
    grad_residual_low = grad_residual.astype(jnp.bfloat16)
    grad_proj = contract_rows(token_attended, grad_residual_low)
    grad_token_att = (
        contract_cols(grad_residual_low, full_proj)
        .astype(jnp.bfloat16)
        .reshape(clip_count, local_len, local_width)
    )
    grad_head_att = lax.all_to_all(grad_token_att, "ctx", split_axis=2, concat_axis=1, tiled=True)
    grad_grouped = (
        grad_head_att.reshape(clip_count, full_len, group_heads, HD)
        .transpose(0, 2, 1, 3)
        .reshape(group_count, full_len, HD)
    )
    grad_q, grad_k, grad_v = lax.map(
        backward_group, (grouped[0], grouped[1], grouped[2], grad_grouped, log_totals)
    )
    grad_heads = jnp.stack([grad_q, grad_k, grad_v]).astype(jnp.bfloat16)
    grad_heads = (
        grad_heads.reshape(3, clip_count, group_heads, full_len, HD)
        .transpose(0, 1, 3, 2, 4)
        .reshape(3, clip_count, full_len, group_heads * HD)
    )
    grad_tokens = (
        lax.all_to_all(grad_heads, "ctx", split_axis=2, concat_axis=3, tiled=True)
        .reshape(3, row_count, local_width)
        .astype(jnp.float32)
    )

    def rotate_rows(moved):
        return rotary(moved, cos_table, sin_table)

    _, rotary_pull = jax.vjp(rotate_rows, jnp.zeros(head_shape, jnp.float32))
    grad_q_pre = rotary_pull(grad_tokens[0].reshape(head_shape))[0].reshape(row_count, local_width)
    grad_k_pre = rotary_pull(grad_tokens[1].reshape(head_shape))[0].reshape(row_count, local_width)
    grad_qkv_low = jnp.stack([grad_q_pre, grad_k_pre, grad_tokens[2]]).astype(jnp.bfloat16)
    grad_b_qkv = jnp.sum(grad_qkv_low.astype(jnp.float32), axis=1)
    grad_qkv = jnp.einsum(
        "rd,cre->cde", normed_one_low, grad_qkv_low, preferred_element_type=jnp.float32
    )
    back_part_one = jnp.einsum(
        "cre,cde->rd", grad_qkv_low, full_qkv, preferred_element_type=jnp.float32
    )
    grad_normed_one = tp_whole(back_part_one)
    _, norm_pull_one = jax.vjp(layer_norm, inputs, norm_gains[0], norm_shifts[0])
    grad_in_norm, grad_gain_one, grad_shift_one = norm_pull_one(grad_normed_one)
    grad_input_rows = grad_residual + grad_in_norm
    norm_vectors = jnp.stack(
        [
            grad_gain_one,
            grad_gain_two,
            grad_shift_one,
            grad_shift_two,
            jnp.sum(grad_residual, axis=0),
            jnp.sum(upstream, axis=0),
        ]
    )
    block_output = block_rows.reshape(clip_count, local_len, width)
    grad_input = grad_input_rows.reshape(clip_count, local_len, width)
    shard_qkv, shard_proj, shard_up, shard_down = (
        lax.psum_scatter(
            grad_qkv.astype(jnp.bfloat16), "fsdp", scatter_dimension=1, tiled=True
        ).astype(jnp.float32),
        lax.psum_scatter(
            grad_proj.astype(jnp.bfloat16), "fsdp", scatter_dimension=1, tiled=True
        ).astype(jnp.float32),
        lax.psum_scatter(
            grad_up.astype(jnp.bfloat16), "fsdp", scatter_dimension=0, tiled=True
        ).astype(jnp.float32),
        lax.psum_scatter(
            grad_down.astype(jnp.bfloat16), "fsdp", scatter_dimension=1, tiled=True
        ).astype(jnp.float32),
    )
    shard_qkv, shard_proj, shard_up, shard_down = (
        lax.psum(shard_qkv.astype(jnp.bfloat16), "ctx").astype(jnp.float32),
        lax.psum(shard_proj.astype(jnp.bfloat16), "ctx").astype(jnp.float32),
        lax.psum(shard_up.astype(jnp.bfloat16), "ctx").astype(jnp.float32),
        lax.psum(shard_down.astype(jnp.bfloat16), "ctx").astype(jnp.float32),
    )
    gains_sum, shifts_sum, outs_sum, bqkv_sum, bup_sum = lax.psum(
        (norm_vectors[0:2], norm_vectors[2:4], norm_vectors[4:6], grad_b_qkv, grad_b_up),
        ("fsdp", "ctx"),
    )
    return (
        block_output,
        grad_input,
        shard_qkv,
        bqkv_sum,
        shard_proj,
        shard_up,
        bup_sum,
        shard_down,
        gains_sum,
        shifts_sum,
        outs_sum,
    )


def solution(mesh):
    in_specs = (
        P("fsdp", "ctx", None),
        P(None, "fsdp", "ctx"),
        P(None, "fsdp", "tp"),
        P(None, "tp"),
        P("tp", "fsdp"),
        P("fsdp", "tp"),
        P("tp"),
        P("tp", "fsdp"),
        P(),
        P(),
        P(),
        P("fsdp", "ctx", None),
    )
    out_specs = (
        P("fsdp", "ctx", None),
        P("fsdp", "ctx", None),
        P(None, "fsdp", "tp"),
        P(None, "tp"),
        P("tp", "fsdp"),
        P("fsdp", "tp"),
        P("tp"),
        P("tp", "fsdp"),
        P(),
        P(),
        P(),
    )
    return jax.shard_map(shards, mesh=mesh, in_specs=in_specs, out_specs=out_specs, check_vma=False)
```

profile of v0, /device:TPU:0, one launch (start us, length us, event | category | flops | bytes accessed | tf_op | source)
XLA Modules:
  0.0 875.1 jit_solution(13437522062420596701)
XLA Ops:
  17.3 22.8 %all-gather.4.cloned.1.call-done = bf16[3,1024,256]{1,2,0:T(8,128)(2,1)} async-done(((bf16[3,512,256]{1,2,0:T(8,128)(2,1)}), bf16[3,1024,256]{1,2,0:T(8,128)(2,1)}) %all-gather.4.cloned.1.call-update) | async-done | bytes 1572880 | tf_op jit(solution)/shard_map/all_gather | solution.py:137
  40.1 3.9 add_bitcast_fusion
  51.5 3.1 pad_maximum_fusion.1
  54.5 3.8 all-to-all-start
  58.3 20.0 %all-to-all-done = bf16[3,2,512,256]{2,1,0,3:T(2,128)(2,1)S(1)} async-done(((bf16[3,2,512,256]{2,1,0,3:T(2,128)(2,1)}), bf16[3,2,512,256]{2,1,0,3:T(2,128)(2,1)S(1)}, u32[]{:S(2)}, u32[]{:S(2)}) %all-to-all-start) | async-done | bytes 1572896 | tf_op jit(solution)/shard_map/all_to_all | solution.py:161
  83.0 27.2 %while.54 = (s32[]{:T(128)}, bf16[2,4,512,64]{2,3,1,0:T(8,128)(2,1)}, f32[2,4,512]{2,1,0:T(4,128)S(1)}, bf16[2,2048,64]{2,1,0:T(8,128)(2,1)S(1)}, bf16[2,2048,64...) while((s32[]{:T(128)}, ...), condition=%wide.region_7.8_spmd, body=%wide.region_2.7_spmd.sunk | while | flops 277904896 | bytes 20156772 | solution.py:168
  84.4 11.4 %while.57 = (s32[]{:T(128)}, bf16[4,512,64]{1,2,0:T(8,128)(2,1)S(1)}, f32[4,512]{1,0:T(4,128)S(1)}, bf16[4,512,64]{2,1,0:T(8,128)(2,1)S(1)}, bf16[2048,64]{1,0:T...) while((s32[]{:T(128)}, bf16[4,512,64]{1,2,0:T(8,128)(2,1)S(1)}, ...), condition=%wide.region_6.6_spmd, body=%wide.region_3.5_spmd.sunk | while | flops 277904896 | bytes 13848681 | solution.py:76
  98.0 11.4 %while.57 = (s32[]{:T(128)}, bf16[4,512,64]{1,2,0:T(8,128)(2,1)S(1)}, f32[4,512]{1,0:T(4,128)S(1)}, bf16[4,512,64]{2,1,0:T(8,128)(2,1)S(1)}, bf16[2048,64]{1,0:T...) while((s32[]{:T(128)}, bf16[4,512,64]{1,2,0:T(8,128)(2,1)S(1)}, ...), condition=%wide.region_6.6_spmd, body=%wide.region_3.5_spmd.sunk | while | flops 277904896 | bytes 13848681 | solution.py:76
  114.4 3.5 all-to-all-start.1
  117.9 9.3 %all_gather.17 = bf16[256,1024]{1,0:T(8,128)(2,1)S(1)} all-gather(bf16[256,512]{1,0:T(8,128)(2,1)S(1)} %copy-done.30), channel_id=1, replica_groups=mesh['fsdp'=2,'ctx'=4,'tp'=4] {'fsdp'}, dimensions={1}, use_global_device_ids=true | all-gather | bytes 786432 | tf_op jit(solution)/shard_map/all_gather | solution.py:138
  135.5 84.2 %all-reduce.22.cloned.1.call-done = bf16[1024,1024]{1,0:T(8,128)(2,1)} async-done(((bf16[1024,1024]{1,0:T(8,128)(2,1)}), bf16[1024,1024]{1,0:T(8,128)(2,1)}) %all-reduce.22.cloned.1.call-update) | async-done | bytes 2097168 | tf_op jit(solution)/shard_map/psum | solution.py:55
  222.2 3.0 multiply_reduce_fusion.2
  225.3 28.2 %all-gather.6.cloned.1.call-done = bf16[1024,1024]{1,0:T(8,128)(2,1)} async-done(((bf16[512,1024]{1,0:T(8,128)(2,1)}), bf16[1024,1024]{1,0:T(8,128)(2,1)}) %all-gather.6.cloned.1.call-update) | async-done | bytes 2097168 | tf_op jit(solution)/shard_map/all_gather | solution.py:139
  253.4 7.4 fusion.69
  260.8 27.1 %all-gather.8.cloned.1.call-done = bf16[1024,1024]{1,0:T(8,128)(2,1)} async-done(((bf16[1024,512]{1,0:T(8,128)(2,1)}), bf16[1024,1024]{1,0:T(8,128)(2,1)}) %all-gather.8.cloned.1.call-update) | async-done | bytes 2097168 | tf_op jit(solution)/shard_map/all_gather | solution.py:140
  287.9 16.0 %convert_reduce_fusion.4 = (f32[1024]{0:T(1024)}, bf16[1024,1024]{1,0:T(8,128)(2,1)S(1)}, f32[1024,1024]{1,0:T(8,128)}) fusion(f32[1024,1024]{1,0:T(8,128)} %fusion.69, f32[1024]{0:T(1024)S(1)} %copy-done.50, bf16[1024,1024]{1,0:T(8,128)(2,1)S(1)} %bitcast.274, bf16[1024,1024]{1,0:T(8,128)(2,1)} %all-gather.8.cloned.1.call-done), kind=kOutput, calls=%fused_computation.82 | convolution fusion | flops 2226125824 | bytes 14688256 | tf_op jit(solution)/shard_map/dot_general | solution.py:49
  305.2 3.7 convolution_convert_fusion.2
  308.9 12.1 %reduce-scatter.7.cloned.1.call-start = ((), (), s32[]{:S(2)}) async-start(), calls=%async_computation.14 | async-start | bytes 786432 | tf_op jit(solution)/shard_map/reduce_scatter | solution.py:266
  321.1 74.2 %all-reduce.24.cloned.1.call-done = bf16[1024,1024]{1,0:T(8,128)(2,1)} async-done(((bf16[1024,1024]{1,0:T(8,128)(2,1)}), bf16[1024,1024]{1,0:T(8,128)(2,1)}) %all-reduce.24.cloned.1.call-update) | async-done | bytes 2097168 | tf_op jit(solution)/shard_map/psum | solution.py:55
  395.3 4.5 convert_reduce_fusion.1
  408.6 4.6 multiply_convert_fusion.1
  414.5 3.8 convolution_convert_fusion
  418.3 3.0 convolution_convert_fusion.6
  422.5 3.5 all-to-all-start.2
  426.0 6.9 convolution_convert_fusion.1
  436.1 103.6 %while.56 = (s32[]{:T(128)}, bf16[2,2048,64]{2,0,1:T(2,128)(2,1)}, bf16[2,2048,64]{1,2,0:T(8,128)(2,1)}, bf16[2,2048,64]{1,2,0:T(8,128)(2,1)}, bf16[2,2048,64]{2...) while((s32[]{:T(128)}, bf16[2,2048,64]{2,0,1:T(2,128)(2,1)}, ...), condition=%wide.region_19.20_spmd, body=%wide.region_15.19_spmd.sunk | while | flops 680164864 | bytes 41838996 | solution.py:217
  440.5 20.1 %while.58 = (s32[]{:T(128)}, f32[2048,64]{0,1:T(8,128)S(1)}, f32[2048,64]{0,1:T(8,128)S(1)}, f32[4,512,64]{1,2,0:T(8,128)}, bf16[4,512,64]{2,1,0:T(8,128)(2,1)S(...) while((s32[]{:T(128)}, f32[2048,64]{0,1:T(8,128)S(1)}, ...), condition=%wide.region_18.18_spmd.clone, body=%wide.region_16.17_spmd.clone.sunk | while | flops 680164864 | bytes 35530900 | solution.py:111
  462.0 25.1 %dynamic_update_slice.47 = bf16[2,2048,64]{2,0,1:T(2,128)(2,1)} dynamic-update-slice(bf16[2,2048,64]{2,0,1:T(2,128)(2,1)} %get-tuple-element.795, f32[1,2048,64]{2,0,1:T(1,128)S(1)} %bitcast.268, s32[]{:T(128)S(6)} %copy.189, s32[]{:T(128)} %constant.78.clone.1..sunk.2, s32[]{:T(128)} %constant.78.clone.1..sunk.2) | dynamic-update-slice | bytes 1048580 | tf_op jit(solution)/shard_map/while/body/jit(dynamic_update_index_in_dim)/dynamic_update_slice | solution.py:217
  492.3 20.1 %while.58 = (s32[]{:T(128)}, f32[2048,64]{0,1:T(8,128)S(1)}, f32[2048,64]{0,1:T(8,128)S(1)}, f32[4,512,64]{1,2,0:T(8,128)}, bf16[4,512,64]{2,1,0:T(8,128)(2,1)S(...) while((s32[]{:T(128)}, f32[2048,64]{0,1:T(8,128)S(1)}, ...), condition=%wide.region_18.18_spmd.clone, body=%wide.region_16.17_spmd.clone.sunk | while | flops 680164864 | bytes 35530900 | solution.py:111
  513.8 25.1 %dynamic_update_slice.47 = bf16[2,2048,64]{2,0,1:T(2,128)(2,1)} dynamic-update-slice(bf16[2,2048,64]{2,0,1:T(2,128)(2,1)} %get-tuple-element.795, f32[1,2048,64]{2,0,1:T(1,128)S(1)} %bitcast.268, s32[]{:T(128)S(6)} %copy.189, s32[]{:T(128)} %constant.78.clone.1..sunk.2, s32[]{:T(128)} %constant.78.clone.1..sunk.2) | dynamic-update-slice | bytes 1048580 | tf_op jit(solution)/shard_map/while/body/jit(dynamic_update_index_in_dim)/dynamic_update_slice | solution.py:217
  539.7 3.6 copy.142
  543.3 3.6 copy.141
  546.8 7.2 fusion.79
  554.0 3.3 reshape.228
  557.3 24.7 %all_to_all.57 = bf16[4,2,98304]{2,1,0:T(2,128)(2,1)} all-to-all(bf16[4,2,98304]{2,1,0:T(2,128)(2,1)} %reshape.228), channel_id=1, replica_groups=mesh['fsdp'=2,'ctx'=4,'tp'=4] {'ctx'}, dimensions={0} | all-to-all | bytes 3145728 | tf_op jit(solution)/shard_map/all_to_all | solution.py:227
  582.0 3.8 reshape.229
  585.8 6.4 copy.92
  601.3 4.9 fusion.61
  606.3 5.4 convolution_convert_fusion.3
  611.7 3.1 bitcast_convert_fusion
  618.7 11.9 %reduce-scatter.5.cloned.1.call-done = bf16[3,512,256]{1,2,0:T(8,128)(2,1)} async-done(((bf16[3,1024,256]{1,2,0:T(8,128)(2,1)}), bf16[3,512,256]{1,2,0:T(8,128)(2,1)}) %reduce-scatter.5.cloned.1.call-update) | async-done | bytes 786448 | tf_op jit(solution)/shard_map/reduce_scatter | solution.py:263
  630.7 157.9 %all-reduce.26.cloned.1.call-done = (bf16[1024,1024]{1,0:T(8,128)(2,1)}, bf16[1024,1024]{1,0:T(8,128)(2,1)}) async-done(((bf16[1024,1024]{1,0:T(8,128)(2,1)}, bf16[1024,1024]{1,0:T(8,128)(2,1)}), (bf16[1024,1024]{1,0:T(8,128)(2,1)}, bf16[1024,1024]{1,0:T(8,128)(2,1)})) %all-reduce.26.cloned.1.call-update) | async-done | bytes 4194320 | tf_op jit(solution)/shard_map/psum | solution.py:55
  788.6 3.1 convert_reduce_fusion
  791.7 2.7 fusion.35
  794.5 26.2 %all-reduce.14 = (f32[3,256]{1,0:T(4,128)}, f32[1024]{0:T(1024)}, f32[2,1024]{1,0:T(2,128)}, f32[2,1024]{1,0:T(2,128)}, f32[2,1024]{1,0:T(2,128)}) all-reduce(f32[3,256]{1,0:T(4,128)S(1)} %convert_reduce_fusion.5, f32[1024]{0:T(1024)S(1)} %copy-done.52, ...), channel_id=1, replica_groups=mesh['fsdp'=2,'ctx'=4,'tp'=4] {'fsdp','ctx'}, use_global_device_ids=true, to_apply=%region_26.27 | all-reduce | flops 7936 | bytes 63488 | tf_op jit(solution)/shard_map/psum | solution.py:282
  820.7 7.1 add_add_fusion.2
  827.9 31.4 %all-reduce.28.cloned.1.call-done = (bf16[3,512,256]{1,2,0:T(8,128)(2,1)}, bf16[256,512]{1,0:T(8,128)(2,1)}, bf16[512,1024]{1,0:T(8,128)(2,1)}, bf16[1024,512]{1,0:T(8,128)(2,1)}) async-done(((bf16[3,512,256]{1,2,0:T(8,128)(2,1)}, bf16[256,512]{1,0:T(8,128)(2,1)}, bf16[512,1024]{1,0:T(8,128)(2,1)}, bf16[1024,512]{1,0:T(8,128)(2,1)}), (bf16[3,512,256]{1,2,0:T(8,128)(2,1)}, bf16[256,512]{1,0:T(8,128)(2,1)}, ...) | async-done | bytes 3145744 | tf_op jit(solution)/shard_map/psum | solution.py:277
  863.7 2.8 convert_element_type.170
  (351 shorter events, 151.5 us)
Async XLA Ops:
  7.2 5.3 copy-start.46
  7.2 5.8 copy-start.47
  7.2 6.4 copy-start.48
  7.2 32.9 %all-gather.4.cloned.1.call-start = ((), (), s32[]{:S(2)}) async-start(), calls=%async_computation.8 | async-start | bytes 2359296 | tf_op jit(solution)/shard_map/all_gather | solution.py:137
  11.7 28.4 %copy-start.55 = (f32[3,256]{1,0:T(4,128)S(1)}, f32[3,256]{1,0:T(4,128)}, u32[]{:S(2)}) copy-start(f32[3,256]{1,0:T(4,128)} %param.23) | copy-start | bytes 9220
  15.0 30.8 %copy-start.15 = (f32[1024,10]{0,1:T(8,128)}, f32[1024,10]{0,1:T(8,128)S(1)}, u32[]{:S(2)}) copy-start(f32[1024,10]{0,1:T(8,128)S(1)} %get-tuple-element.436) | copy-start | bytes 122884
  15.0 30.8 %copy-start.17 = (f32[1024,10]{0,1:T(8,128)}, f32[1024,10]{0,1:T(8,128)S(1)}, u32[]{:S(2)}) copy-start(f32[1024,10]{0,1:T(8,128)S(1)} %get-tuple-element.437) | copy-start | bytes 122884
  15.0 30.8 %copy-start.19 = (f32[1024,10]{0,1:T(8,128)}, f32[1024,10]{0,1:T(8,128)S(1)}, u32[]{:S(2)}) copy-start(f32[1024,10]{0,1:T(8,128)S(1)} %get-tuple-element.438) | copy-start | bytes 122884
  15.1 30.8 %copy-start.21 = (f32[1024,10]{0,1:T(8,128)}, f32[1024,10]{0,1:T(8,128)S(1)}, u32[]{:S(2)}) copy-start(f32[1024,10]{0,1:T(8,128)S(1)} %get-tuple-element.449) | copy-start | bytes 122884
  15.1 30.8 %copy-start.23 = (f32[1024,10]{0,1:T(8,128)}, f32[1024,10]{0,1:T(8,128)S(1)}, u32[]{:S(2)}) copy-start(f32[1024,10]{0,1:T(8,128)S(1)} %get-tuple-element.450) | copy-start | bytes 122884
  15.1 30.8 %copy-start.25 = (f32[1024,10]{0,1:T(8,128)}, f32[1024,10]{0,1:T(8,128)S(1)}, u32[]{:S(2)}) copy-start(f32[1024,10]{0,1:T(8,128)S(1)} %get-tuple-element.451) | copy-start | bytes 122884
  54.5 23.8 %all-to-all-start = ((bf16[3,2,512,256]{2,1,0,3:T(2,128)(2,1)}), bf16[3,2,512,256]{2,1,0,3:T(2,128)(2,1)S(1)}, u32[]{:S(2)}, u32[]{:S(2)}) async-start(bf16[3,2,512,256]{2,1,0,3:T(2,128)(2,1)} %pad_maximum_fusion.1), calls=%async_computation | async-start | bytes 3145728 | tf_op jit(solution)/shard_map/all_to_all | solution.py:161
  84.4 11.4 %copy-start.28 = (bf16[2,4,512,64]{2,3,1,0:T(8,128)(2,1)S(1)}, bf16[2,4,512,64]{2,3,1,0:T(8,128)(2,1)}, u32[]{:S(2)}) copy-start(bf16[2,4,512,64]{2,3,1,0:T(8,128)(2,1)} %get-tuple-element.762) | copy-start | bytes 1572868 | tf_op jit(solution)/shard_map/while
  98.0 11.4 %copy-start.28 = (bf16[2,4,512,64]{2,3,1,0:T(8,128)(2,1)S(1)}, bf16[2,4,512,64]{2,3,1,0:T(8,128)(2,1)}, u32[]{:S(2)}) copy-start(bf16[2,4,512,64]{2,3,1,0:T(8,128)(2,1)} %get-tuple-element.762) | copy-start | bytes 1572868 | tf_op jit(solution)/shard_map/while
  110.2 19.6 %copy-start.5 = (bf16[2,2048,64]{2,1,0:T(8,128)(2,1)}, bf16[2,2048,64]{2,1,0:T(8,128)(2,1)S(1)}, u32[]{:S(2)}) copy-start(bf16[2,2048,64]{2,1,0:T(8,128)(2,1)S(1)} %get-tuple-element.841) | copy-start | bytes 1572868
  110.3 7.7 copy-start.30
  114.4 12.8 %all-to-all-start.1 = ((bf16[4,2,32768]{2,1,0:T(2,128)(2,1)}), bf16[4,2,32768]{2,1,0:T(2,128)(2,1)S(1)}, u32[]{:S(2)}, u32[]{:S(2)}) async-start(bf16[4,2,32768]{2,1,0:T(2,128)(2,1)} %reshape.226), calls=%async_computation.1 | async-start | bytes 1048576 | tf_op jit(solution)/shard_map/all_to_all | solution.py:174
  117.9 101.8 %all-reduce.22.cloned.1.call-start = ((), (), s32[]{:S(2)}) async-start(), calls=%async_computation.9 | async-start | bytes 4194304 | tf_op jit(solution)/shard_map/psum | solution.py:55
  129.9 89.8 %copy-start.1 = (bf16[2,512,1024]{2,1,0:T(8,128)(2,1)S(1)}, bf16[2,512,1024]{2,1,0:T(8,128)(2,1)}, u32[]{:S(2)}) copy-start(bf16[2,512,1024]{2,1,0:T(8,128)(2,1)} %param.20) | copy-start | bytes 6291460
  133.2 120.2 %all-gather.6.cloned.1.call-start = ((), (), s32[]{:S(2)}) async-start(), calls=%async_computation.10 | async-start | bytes 3145728 | tf_op jit(solution)/shard_map/all_gather | solution.py:139
  134.0 154.0 %all-gather.8.cloned.1.call-start = ((), (), s32[]{:S(2)}) async-start(), calls=%async_computation.11 | async-start | bytes 3145728 | tf_op jit(solution)/shard_map/all_gather | solution.py:140
  134.5 260.7 %all-reduce.24.cloned.1.call-start = ((), (), s32[]{:S(2)}) async-start(), calls=%async_computation.12 | async-start | bytes 4194304 | tf_op jit(solution)/shard_map/psum | solution.py:55
  135.5 89.7 %copy-start.36 = (f32[1,1024]{1,0:T(1,128)}, f32[1,1024]{1,0:T(1,128)S(1)}, u32[]{:S(2)}) copy-start(f32[1,1024]{1,0:T(1,128)S(1)} %get-tuple-element.442) | copy-start | bytes 12292
  222.2 31.2 %copy-start.35 = (f32[1,1024]{1,0:T(1,128)S(1)}, f32[1,1024]{1,0:T(1,128)}, u32[]{:S(2)}) copy-start(f32[1,1024]{1,0:T(1,128)} %get-tuple-element.443) | copy-start | bytes 12292
  222.2 31.2 %copy-start.51 = (f32[1,1024]{1,0:T(1,128)S(1)}, f32[1,1024]{1,0:T(1,128)}, u32[]{:S(2)}) copy-start(f32[1,1024]{1,0:T(1,128)} %get-tuple-element.445) | copy-start | bytes 12292
  253.4 34.5 %copy-start.10 = (bf16[2,512,1024]{2,1,0:T(8,128)(2,1)S(1)}, bf16[2,512,1024]{2,1,0:T(8,128)(2,1)}, u32[]{:S(2)}) copy-start(bf16[2,512,1024]{2,1,0:T(8,128)(2,1)} %param.31) | copy-start | bytes 6291460
  253.4 34.5 %copy-start.50 = (f32[1024]{0:T(1024)S(1)}, f32[1024]{0:T(1024)}, u32[]{:S(2)}) copy-start(f32[1024]{0:T(1024)} %param.26) | copy-start | bytes 12292
  287.9 17.3 %copy-start.53 = (bf16[1024,1024]{1,0:T(8,128)(2,1)S(1)}, bf16[1024,1024]{1,0:T(8,128)(2,1)}, u32[]{:S(2)}) copy-start(bf16[1024,1024]{1,0:T(8,128)(2,1)} %all-gather.6.cloned.1.call-done) | copy-start | bytes 6291460
  308.9 309.7 %reduce-scatter.7.cloned.1.call-start = ((), (), s32[]{:S(2)}) async-start(), calls=%async_computation.14 | async-start | bytes 786432 | tf_op jit(solution)/shard_map/reduce_scatter | solution.py:266
  408.5 210.2 %reduce-scatter.11.cloned.1.call-start = ((), (), s32[]{:S(2)}) async-start(), calls=%async_computation.16 | async-start | bytes 3145728 | tf_op jit(solution)/shard_map/reduce_scatter | solution.py:272
  422.5 12.3 %all-to-all-start.2 = ((bf16[2,512,256]{1,0,2:T(2,128)(2,1)}), bf16[2,512,256]{1,0,2:T(2,128)(2,1)S(1)}, u32[]{:S(2)}, u32[]{:S(2)}) async-start(bf16[2,512,256]{1,0,2:T(2,128)(2,1)} %copy.83), calls=%async_computation.2 | async-start | bytes 1048576 | tf_op jit(solution)/shard_map/all_to_all | solution.py:211
  426.0 192.7 %reduce-scatter.9.cloned.1.call-start = ((), (), s32[]{:S(2)}) async-start(), calls=%async_computation.15 | async-start | bytes 3145728 | tf_op jit(solution)/shard_map/reduce_scatter | solution.py:269
  432.9 197.7 %reduce-scatter.5.cloned.1.call-start = ((), (), s32[]{:S(2)}) async-start(), calls=%async_computation.13 | async-start | bytes 2359296 | tf_op jit(solution)/shard_map/reduce_scatter | solution.py:263
  606.2 182.3 %all-reduce.26.cloned.1.call-start = ((), (), s32[]{:S(2)}) async-start(), calls=%async_computation.17 | async-start | bytes 8388608 | tf_op jit(solution)/shard_map/psum | solution.py:55
  606.3 5.4 copy-start.14
  606.3 5.4 copy-start.54
  614.8 173.7 %copy-start.2 = (bf16[2,512,1024]{2,1,0:T(8,128)(2,1)S(1)}, bf16[2,512,1024]{2,1,0:T(8,128)(2,1)}, u32[]{:S(2)}) copy-start(bf16[2,512,1024]{2,1,0:T(8,128)(2,1)} %param.20) | copy-start | bytes 6291460
  614.8 173.7 %copy-start.32 = (f32[1,4,2,128]{3,1,2,0:T(4,128)S(1)}, f32[1,4,2,128]{3,1,2,0:T(4,128)}, u32[]{:S(2)}) copy-start(f32[1,4,2,128]{3,1,2,0:T(4,128)} %copy-done.31) | copy-start | bytes 12292
  614.9 173.7 %copy-start.34 = (f32[1,1024]{1,0:T(1,128)S(1)}, f32[1,1024]{1,0:T(1,128)}, u32[]{:S(2)}) copy-start(f32[1,1024]{1,0:T(1,128)} %copy-done.33) | copy-start | bytes 12292
  614.9 244.4 %all-reduce.28.cloned.1.call-start = ((), (), s32[]{:S(2)}) async-start(), calls=%async_computation.18 | async-start | bytes 6291456 | tf_op jit(solution)/shard_map/psum | solution.py:277
  617.3 174.4 %copy-start.41 = (f32[1,4,2,128]{3,1,2,0:T(4,128)S(1)}, f32[1,4,2,128]{3,1,2,0:T(4,128)}, u32[]{:S(2)}) copy-start(f32[1,4,2,128]{3,1,2,0:T(4,128)} %copy-done.40) | copy-start | bytes 12292
  617.3 174.4 %copy-start.44 = (f32[1024]{0:T(1024)S(1)}, f32[1024]{0:T(1024)}, u32[]{:S(2)}) copy-start(f32[1024]{0:T(1024)} %get-tuple-element.296) | copy-start | bytes 12292
  617.3 174.4 %copy-start.39 = (f32[1024]{0:T(1024)S(1)}, f32[1024]{0:T(1024)}, u32[]{:S(2)}) copy-start(f32[1024]{0:T(1024)} %copy-done.38) | copy-start | bytes 12292
  788.5 5.9 copy-start.43
  788.5 5.9 copy-start.52
  788.6 32.2 %copy-start.37 = (f32[1,1024]{1,0:T(1,128)S(1)}, f32[1,1024]{1,0:T(1,128)}, u32[]{:S(2)}) copy-start(f32[1,1024]{1,0:T(1,128)} %copy-done.36) | copy-start | bytes 12292
  788.6 32.2 %copy-start.45 = (f32[1,1024]{1,0:T(1,128)S(1)}, f32[1,1024]{1,0:T(1,128)}, u32[]{:S(2)}) copy-start(f32[1,1024]{1,0:T(1,128)} %get-tuple-element.441) | copy-start | bytes 12292
  859.2 7.2 copy-start.27
  (25 other events, 62.0 us)
Sparse Core Ops, SparseCore 0:
  10.1 29.8 all-gather.3
  133.3 86.3 all-reduce.21
  221.2 32.1 all-gather.5
  254.8 33.0 all-gather.7
  309.1 86.1 all-reduce.23
  408.7 13.6 reduce-scatter.6
  424.6 31.8 reduce-scatter.10
  458.8 31.8 reduce-scatter.8
  606.3 24.2 reduce-scatter.4
  633.5 155.0 all-reduce.25
  791.1 68.0 all-reduce.27
where the time goes:
time: 888 us; the launch traced here: 875 us
  waiting for transfers between devices  461 us (52%)
  local copies, waits for them, and re-layouts  130 us (15%)
  matrix products  113 us (13%)
  other arithmetic  71.1 us (8%)
  blocking collectives  60.2 us (7%)
  starting transfers between devices  23.8 us (3%)
  between operations  15.3 us (2%)
    psum x3, waiting for transfers between devices, tp_whole(): return lax.psum(partial_sum.astype(jnp.bfloat16), 'tp').astype(jnp.float32)  316 us
    dynamic_update_slice x4, local copies, waits for them, and re-layouts, shards(): lax.map(backward_group, (grouped[0], grouped[1], grouped[2], grad_grouped...  51.9 us
    psum x1, waiting for transfers between devices, shards(): lax.psum(shard_qkv.astype(jnp.bfloat16), 'ctx').astype(jnp.float32)  31.4 us
    unnamed x122, local copies, waits for them, and re-layouts  28.2 us
    all_gather x1, waiting for transfers between devices, shards(): lax.all_gather(w_up, 'fsdp', axis=0, tiled=True)  28.2 us
    all_gather x1, waiting for transfers between devices, shards(): lax.all_gather(w_down, 'fsdp', axis=1, tiled=True)  27.1 us
    psum x1, blocking collectives, shards(): lax.psum((norm_vectors[0:2], norm_vectors[2:4], norm_vectors[4:6], grad_b...  26.2 us
    all_to_all x1, blocking collectives, shards(): lax.all_to_all(grad_heads, 'ctx', split_axis=2, concat_axis=3, tiled=True)  24.7 us
  transfers between devices with their start and end apart: 14, of which 10 were waited for; matrix products, arithmetic and copies ran while one was open for 24% of the time, Pallas kernels for 0%

commit v1 on v0

--- a/solution.py
+++ b/solution.py
@@ -52,7 +52,9 @@
 
 
 def tp_whole(partial_sum):
-    return lax.psum(partial_sum.astype(jnp.bfloat16), "tp").astype(jnp.float32)
+    return jnp.sum(lax.all_gather(partial_sum.astype(jnp.bfloat16), "tp"), axis=0).astype(
+        jnp.float32
+    )
 
 
 def attend_group(operands):

time: 888 us -> 1250 us (1.41)
  waiting for transfers between devices: 461 us -> 801 us
  other arithmetic: 71.1 us -> 105 us
    all_gather x0 -> x4, waiting for transfers between devices: none -> 565 us  [tp_whole(): lax.all_gather(partial_sum.astype(jnp.bfloat16), 'tp')]
    psum x3 -> x0, waiting for transfers between devices: 316 us -> none  [tp_whole(): return lax.psum(partial_sum.astype(jnp.bfloat16), 'tp').astype(jnp.float32)]
    reduce_scatter x1, waiting for transfers between devices: 0.02 us -> 34.2 us  [shards(): lax.psum_scatter(grad_up.astype(jnp.bfloat16), 'fsdp', scatter_dimension=...]
    reduce_sum x1 -> x4, other arithmetic: 2.12 us -> 30.1 us  [tp_whole(): jnp.sum(lax.all_gather(partial_sum.astype(jnp.bfloat16), 'tp'), axis=0)]
    reduce_scatter x1, waiting for transfers between devices: 0.02 us -> 17.5 us  [shards(): lax.psum_scatter(grad_proj.astype(jnp.bfloat16), 'fsdp', scatter_dimensio...]
    reduce_scatter x1, waiting for transfers between devices: 11.9 us -> 28.8 us  [shards(): lax.psum_scatter(grad_qkv.astype(jnp.bfloat16), 'fsdp', scatter_dimension...]
    reduce_scatter x1, waiting for transfers between devices: 0.02 us -> 13.9 us  [shards(): lax.psum_scatter(grad_down.astype(jnp.bfloat16), 'fsdp', scatter_dimensio...]
    psum x1, waiting for transfers between devices: 31.4 us -> 44.8 us  [shards(): lax.psum(shard_qkv.astype(jnp.bfloat16), 'ctx').astype(jnp.float32)]
  transfers between devices with their start and end apart: 14 -> 15, of which waited for: 10 -> 14; matrix products, arithmetic and copies ran while one was open for 24% -> 6% of each run, Pallas kernels for 0% -> 0%
where the time goes in v1:
time: 1250 us; the launch traced here: 1230 us
  waiting for transfers between devices  801 us (64%)
  local copies, waits for them, and re-layouts  128 us (10%)
  matrix products  113 us (9%)
  other arithmetic  105 us (8%)
  blocking collectives  58.8 us (5%)
  between operations  15.4 us (1%)
    all_gather x4, waiting for transfers between devices, tp_whole(): lax.all_gather(partial_sum.astype(jnp.bfloat16), 'tp')  565 us
    dynamic_update_slice x4, local copies, waits for them, and re-layouts, shards(): lax.map(backward_group, (grouped[0], grouped[1], grouped[2], grad_grouped...  51.9 us
    psum x1, waiting for transfers between devices, shards(): lax.psum(shard_qkv.astype(jnp.bfloat16), 'ctx').astype(jnp.float32)  44.8 us
    reduce_scatter x1, waiting for transfers between devices, shards(): lax.psum_scatter(grad_up.astype(jnp.bfloat16), 'fsdp', scatter_dimension=...  34.2 us
    reduce_sum x4, other arithmetic, tp_whole(): jnp.sum(lax.all_gather(partial_sum.astype(jnp.bfloat16), 'tp'), axis=0)  30.1 us
    reduce_scatter x1, waiting for transfers between devices, shards(): lax.psum_scatter(grad_qkv.astype(jnp.bfloat16), 'fsdp', scatter_dimension...  28.8 us
    unnamed x132, local copies, waits for them, and re-layouts  28.1 us
    all_gather x1, waiting for transfers between devices, shards(): lax.all_gather(w_down, 'fsdp', axis=1, tiled=True)  28 us
  transfers between devices with their start and end apart: 15, of which 14 were waited for; matrix products, arithmetic and copies ran while one was open for 6% of the time, Pallas kernels for 0%

profile of v1, /device:TPU:0, one launch (start us, length us, event | category | flops | bytes accessed | tf_op | source)
XLA Modules:
  0.0 1234.4 jit_solution(3005982965014301354)
XLA Ops:
  17.3 22.8 %all-gather.12.cloned.1.call-done = bf16[3,1024,256]{1,2,0:T(8,128)(2,1)} async-done(((bf16[3,512,256]{1,2,0:T(8,128)(2,1)}), bf16[3,1024,256]{1,2,0:T(8,128)(2,1)}) %all-gather.12.cloned.1.call-update) | async-done | bytes 1572880 | tf_op jit(solution)/shard_map/all_gather | solution.py:139
  40.1 3.9 add_bitcast_fusion
  54.5 4.0 all-to-all-start
  58.6 20.0 %all-to-all-done = bf16[3,2,512,256]{2,1,0,3:T(2,128)(2,1)S(1)} async-done(((bf16[3,2,512,256]{2,1,0,3:T(2,128)(2,1)}), bf16[3,2,512,256]{2,1,0,3:T(2,128)(2,1)S(1)}, u32[]{:S(2)}, u32[]{:S(2)}) %all-to-all-start) | async-done | bytes 1572896 | tf_op jit(solution)/shard_map/all_to_all | solution.py:163
  83.3 27.2 %while.54 = (s32[]{:T(128)}, bf16[2,4,512,64]{2,3,1,0:T(8,128)(2,1)}, f32[2,4,512]{2,1,0:T(4,128)S(1)}, bf16[2,2048,64]{2,1,0:T(8,128)(2,1)S(1)}, bf16[2,2048,64...) while((s32[]{:T(128)}, ...), condition=%wide.region_7.8_spmd, body=%wide.region_2.7_spmd.sunk | while | flops 277904896 | bytes 20156772 | solution.py:170
  84.6 11.4 while.57
  98.2 11.4 while.57
  114.6 3.5 all-to-all-start.1
  118.2 9.3 all_gather.41
  133.5 148.6 %all-gather.18.cloned.1.call-done = bf16[4096,1024]{1,0:T(8,128)(2,1)} async-done(((bf16[1024,1024]{1,0:T(8,128)(2,1)}), bf16[4096,1024]{1,0:T(8,128)(2,1)}) %all-gather.18.cloned.1.call-update) | async-done | bytes 8388624 | tf_op jit(solution)/shard_map/all_gather | solution.py:55
  282.0 7.6 reduce_sum.221
  297.8 17.1 %all-gather.14.cloned.1.call-done = bf16[1024,1024]{1,0:T(8,128)(2,1)} async-done(((bf16[512,1024]{1,0:T(8,128)(2,1)}), bf16[1024,1024]{1,0:T(8,128)(2,1)}) %all-gather.14.cloned.1.call-update) | async-done | bytes 2097168 | tf_op jit(solution)/shard_map/all_gather | solution.py:141
  314.9 6.5 fusion.85
  321.4 28.0 %all-gather.16.cloned.1.call-done = bf16[1024,1024]{1,0:T(8,128)(2,1)} async-done(((bf16[1024,512]{1,0:T(8,128)(2,1)}), bf16[1024,1024]{1,0:T(8,128)(2,1)}) %all-gather.16.cloned.1.call-update) | async-done | bytes 2097168 | tf_op jit(solution)/shard_map/all_gather | solution.py:142
  349.4 15.7 %convert_reduce_fusion.2 = (f32[1024]{0:T(1024)}, bf16[1024,1024]{1,0:T(8,128)(2,1)}, f32[1024,1024]{1,0:T(8,128)S(1)}) fusion(f32[1024,1024]{1,0:T(8,128)} %fusion.85, f32[1024]{0:T(1024)S(1)} %copy-done.56, bf16[1024,1024]{1,0:T(8,128)(2,1)} %bitcast.298, bf16[1024,1024]{1,0:T(8,128)(2,1)} %all-gather.16.cloned.1.call-done), kind=kOutput, calls=%fused_computation.85 | convolution fusion | flops 2226125824 | bytes 14688256 | tf_op jit(solution)/shard_map/dot_general | solution.py:49
  367.6 3.7 convolution_convert_fusion.3
  371.6 5.9 convolution_convert_fusion.2
  377.6 143.6 %all-gather.20.cloned.1.call-done = bf16[4096,1024]{1,0:T(8,128)(2,1)} async-done(((bf16[1024,1024]{1,0:T(8,128)(2,1)}), bf16[4096,1024]{1,0:T(8,128)(2,1)}) %all-gather.20.cloned.1.call-update) | async-done | bytes 8388624 | tf_op jit(solution)/shard_map/all_gather | solution.py:55
  521.1 7.5 reduce_sum.227
  528.6 142.3 %all-gather.22.cloned.1.call-done = bf16[4096,1024]{1,0:T(8,128)(2,1)} async-done(((bf16[1024,1024]{1,0:T(8,128)(2,1)}), bf16[4096,1024]{1,0:T(8,128)(2,1)}) %all-gather.22.cloned.1.call-update) | async-done | bytes 8388624 | tf_op jit(solution)/shard_map/all_gather | solution.py:55
  671.0 7.5 reduce_sum.228
  678.4 5.5 multiply_reduce_fusion.2
  690.9 5.0 convert_reduce_fusion.4
  701.8 8.3 all-to-all-done.2
  711.5 103.5 %while.56 = (s32[]{:T(128)}, bf16[2,2048,64]{2,0,1:T(2,128)(2,1)}, bf16[2,2048,64]{1,2,0:T(8,128)(2,1)}, bf16[2,2048,64]{1,2,0:T(8,128)(2,1)}, bf16[2,2048,64]{2...) while((s32[]{:T(128)}, bf16[2,2048,64]{2,0,1:T(2,128)(2,1)}, ...), condition=%wide.region_19.20_spmd, body=%wide.region_15.19_spmd.sunk | while | flops 680164864 | bytes 41838996 | solution.py:219
  715.8 20.0 %while.58 = (s32[]{:T(128)}, f32[2048,64]{0,1:T(8,128)S(1)}, f32[2048,64]{0,1:T(8,128)S(1)}, f32[4,512,64]{1,2,0:T(8,128)}, bf16[4,512,64]{2,1,0:T(8,128)(2,1)S(...) while((s32[]{:T(128)}, f32[2048,64]{0,1:T(8,128)S(1)}, ...), condition=%wide.region_18.18_spmd.clone, body=%wide.region_16.17_spmd.clone.sunk | while | flops 680164864 | bytes 35530900 | solution.py:113
  737.2 25.1 %dynamic_update_slice.47 = bf16[2,2048,64]{2,0,1:T(2,128)(2,1)} dynamic-update-slice(bf16[2,2048,64]{2,0,1:T(2,128)(2,1)} %get-tuple-element.803, f32[1,2048,64]{2,0,1:T(1,128)S(1)} %bitcast.284, s32[]{:T(128)S(6)} %copy.191, s32[]{:T(128)} %constant.78.clone.1..sunk.2, s32[]{:T(128)} %constant.78.clone.1..sunk.2) | dynamic-update-slice | bytes 1048580 | tf_op jit(solution)/shard_map/while/body/jit(dynamic_update_index_in_dim)/dynamic_update_slice | solution.py:219
  767.6 20.0 %while.58 = (s32[]{:T(128)}, f32[2048,64]{0,1:T(8,128)S(1)}, f32[2048,64]{0,1:T(8,128)S(1)}, f32[4,512,64]{1,2,0:T(8,128)}, bf16[4,512,64]{2,1,0:T(8,128)(2,1)S(...) while((s32[]{:T(128)}, f32[2048,64]{0,1:T(8,128)S(1)}, ...), condition=%wide.region_18.18_spmd.clone, body=%wide.region_16.17_spmd.clone.sunk | while | flops 680164864 | bytes 35530900 | solution.py:113
  789.0 25.1 %dynamic_update_slice.47 = bf16[2,2048,64]{2,0,1:T(2,128)(2,1)} dynamic-update-slice(bf16[2,2048,64]{2,0,1:T(2,128)(2,1)} %get-tuple-element.803, f32[1,2048,64]{2,0,1:T(1,128)S(1)} %bitcast.284, s32[]{:T(128)S(6)} %copy.191, s32[]{:T(128)} %constant.78.clone.1..sunk.2, s32[]{:T(128)} %constant.78.clone.1..sunk.2) | dynamic-update-slice | bytes 1048580 | tf_op jit(solution)/shard_map/while/body/jit(dynamic_update_index_in_dim)/dynamic_update_slice | solution.py:219
  814.9 3.6 copy.146
  818.5 3.6 copy.145
  822.1 7.2 fusion.84
  832.6 24.6 %all_to_all.57 = bf16[4,2,98304]{2,1,0:T(2,128)(2,1)} all-to-all(bf16[4,2,98304]{2,1,0:T(2,128)(2,1)} %reshape.506), channel_id=1, replica_groups=mesh['fsdp'=2,'ctx'=4,'tp'=4] {'ctx'}, dimensions={0} | all-to-all | bytes 3145728 | tf_op jit(solution)/shard_map/all_to_all | solution.py:229
  857.2 3.8 reshape.507
  861.0 6.4 copy.92
  882.3 4.8 bitcast_convert_fusion
  887.2 5.3 convolution_convert_fusion
  892.8 6.6 convolution_convert_fusion.1
  899.4 4.6 fusion.63
  904.1 130.1 %all-gather.24.cloned.1.call-done = bf16[4096,1024]{1,0:T(8,128)(2,1)} async-done(((bf16[1024,1024]{1,0:T(8,128)(2,1)}), bf16[4096,1024]{1,0:T(8,128)(2,1)}) %all-gather.24.cloned.1.call-update) | async-done | bytes 8388624 | tf_op jit(solution)/shard_map/all_gather | solution.py:55
  1034.2 7.6 reduce_sum.235
  1047.4 3.6 fusion.66
  1052.6 13.9 %reduce-scatter.11.cloned.1.call-done = bf16[1024,512]{1,0:T(8,128)(2,1)} async-done(((bf16[1024,1024]{1,0:T(8,128)(2,1)}), bf16[1024,512]{1,0:T(8,128)(2,1)}) %reduce-scatter.11.cloned.1.call-update) | async-done | bytes 1048592 | tf_op jit(solution)/shard_map/reduce_scatter | solution.py:274
  1066.5 34.2 %reduce-scatter.9.cloned.1.call-done = bf16[512,1024]{1,0:T(8,128)(2,1)} async-done(((bf16[1024,1024]{1,0:T(8,128)(2,1)}), bf16[512,1024]{1,0:T(8,128)(2,1)}) %reduce-scatter.9.cloned.1.call-update) | async-done | bytes 1048592 | tf_op jit(solution)/shard_map/reduce_scatter | solution.py:271
  1100.7 28.8 %reduce-scatter.5.cloned.1.call-done = bf16[3,512,256]{1,2,0:T(8,128)(2,1)} async-done(((bf16[3,1024,256]{1,2,0:T(8,128)(2,1)}), bf16[3,512,256]{1,2,0:T(8,128)(2,1)}) %reduce-scatter.5.cloned.1.call-update) | async-done | bytes 786448 | tf_op jit(solution)/shard_map/reduce_scatter | solution.py:265
  1129.6 17.5 %reduce-scatter.7.cloned.1.call-done = bf16[256,512]{1,0:T(8,128)(2,1)} async-done(((bf16[256,1024]{1,0:T(8,128)(2,1)}), bf16[256,512]{1,0:T(8,128)(2,1)}) %reduce-scatter.7.cloned.1.call-update) | async-done | bytes 262160 | tf_op jit(solution)/shard_map/reduce_scatter | solution.py:268
  1148.8 24.9 %all-reduce.14 = (f32[3,256]{1,0:T(4,128)}, f32[1024]{0:T(1024)}, f32[2,1024]{1,0:T(2,128)}, f32[2,1024]{1,0:T(2,128)}, f32[2,1024]{1,0:T(2,128)}) all-reduce(f32[3,256]{1,0:T(4,128)S(1)} %convert_reduce_fusion.3, f32[1024]{0:T(1024)S(1)} %copy-done.57, ...), channel_id=1, replica_groups=mesh['fsdp'=2,'ctx'=4,'tp'=4] {'fsdp','ctx'}, use_global_device_ids=true, to_apply=%region_26.27 | all-reduce | flops 7936 | bytes 63488 | tf_op jit(solution)/shard_map/psum | solution.py:284
  1173.7 44.8 %all-reduce.18.cloned.1.call-done = (bf16[3,512,256]{1,2,0:T(8,128)(2,1)}, bf16[256,512]{1,0:T(8,128)(2,1)}, bf16[512,1024]{1,0:T(8,128)(2,1)}, bf16[1024,512]{1,0:T(8,128)(2,1)}) async-done(((bf16[3,512,256]{1,2,0:T(8,128)(2,1)}, bf16[256,512]{1,0:T(8,128)(2,1)}, bf16[512,1024]{1,0:T(8,128)(2,1)}, bf16[1024,512]{1,0:T(8,128)(2,1)}), (bf16[3,512,256]{1,2,0:T(8,128)(2,1)}, bf16[256,512]{1,0:T(8,128)(2,1)}, ...) | async-done | bytes 3145744 | tf_op jit(solution)/shard_map/psum | solution.py:279
  (371 shorter events, 176.2 us)
Async XLA Ops:
  7.2 4.5 copy-start
  7.2 5.8 copy-start.52
  7.2 5.8 copy-start.53
  7.2 6.4 copy-start.54
  7.2 32.9 %all-gather.12.cloned.1.call-start = ((), (), s32[]{:S(2)}) async-start(), calls=%async_computation.8 | async-start | bytes 2359296 | tf_op jit(solution)/shard_map/all_gather | solution.py:139
  11.7 28.4 %copy-start.59 = (f32[3,256]{1,0:T(4,128)S(1)}, f32[3,256]{1,0:T(4,128)}, u32[]{:S(2)}) copy-start(f32[3,256]{1,0:T(4,128)} %param.23) | copy-start | bytes 9220
  15.1 30.8 %copy-start.19 = (f32[1024,10]{0,1:T(8,128)}, f32[1024,10]{0,1:T(8,128)S(1)}, u32[]{:S(2)}) copy-start(f32[1024,10]{0,1:T(8,128)S(1)} %get-tuple-element.436) | copy-start | bytes 122884
  15.1 30.8 %copy-start.21 = (f32[1024,10]{0,1:T(8,128)}, f32[1024,10]{0,1:T(8,128)S(1)}, u32[]{:S(2)}) copy-start(f32[1024,10]{0,1:T(8,128)S(1)} %get-tuple-element.437) | copy-start | bytes 122884
  15.1 30.8 %copy-start.23 = (f32[1024,10]{0,1:T(8,128)}, f32[1024,10]{0,1:T(8,128)S(1)}, u32[]{:S(2)}) copy-start(f32[1024,10]{0,1:T(8,128)S(1)} %get-tuple-element.438) | copy-start | bytes 122884
  15.1 30.8 %copy-start.25 = (f32[1024,10]{0,1:T(8,128)}, f32[1024,10]{0,1:T(8,128)S(1)}, u32[]{:S(2)}) copy-start(f32[1024,10]{0,1:T(8,128)S(1)} %get-tuple-element.457) | copy-start | bytes 122884
  15.1 30.8 %copy-start.27 = (f32[1024,10]{0,1:T(8,128)}, f32[1024,10]{0,1:T(8,128)S(1)}, u32[]{:S(2)}) copy-start(f32[1024,10]{0,1:T(8,128)S(1)} %get-tuple-element.458) | copy-start | bytes 122884
  15.1 30.8 %copy-start.29 = (f32[1024,10]{0,1:T(8,128)}, f32[1024,10]{0,1:T(8,128)S(1)}, u32[]{:S(2)}) copy-start(f32[1024,10]{0,1:T(8,128)S(1)} %get-tuple-element.459) | copy-start | bytes 122884
  54.5 24.0 %all-to-all-start = ((bf16[3,2,512,256]{2,1,0,3:T(2,128)(2,1)}), bf16[3,2,512,256]{2,1,0,3:T(2,128)(2,1)S(1)}, u32[]{:S(2)}, u32[]{:S(2)}) async-start(bf16[3,2,512,256]{2,1,0,3:T(2,128)(2,1)} %pad_maximum_fusion.1), calls=%async_computation | async-start | bytes 3145728 | tf_op jit(solution)/shard_map/all_to_all | solution.py:163
  84.6 11.4 copy-start.37
  98.2 11.4 copy-start.37
  110.5 18.6 %copy-start.9 = (bf16[2,2048,64]{2,1,0:T(8,128)(2,1)}, bf16[2,2048,64]{2,1,0:T(8,128)(2,1)S(1)}, u32[]{:S(2)}) copy-start(bf16[2,2048,64]{2,1,0:T(8,128)(2,1)S(1)} %get-tuple-element.847) | copy-start | bytes 1572868
  110.5 7.7 copy-start.39
  114.6 12.8 %all-to-all-start.1 = ((bf16[4,2,32768]{2,1,0:T(2,128)(2,1)}), bf16[4,2,32768]{2,1,0:T(2,128)(2,1)S(1)}, u32[]{:S(2)}, u32[]{:S(2)}) async-start(bf16[4,2,32768]{2,1,0:T(2,128)(2,1)} %reshape.504), calls=%async_computation.1 | async-start | bytes 1048576 | tf_op jit(solution)/shard_map/all_to_all | solution.py:176
  118.1 163.9 %all-gather.18.cloned.1.call-start = ((), (), s32[]{:S(2)}) async-start(), calls=%async_computation.15 | async-start | bytes 10485760 | tf_op jit(solution)/shard_map/all_gather | solution.py:55
  129.0 4.4 copy-start.55
  132.1 182.8 %all-gather.14.cloned.1.call-start = ((), (), s32[]{:S(2)}) async-start(), calls=%async_computation.9 | async-start | bytes 3145728 | tf_op jit(solution)/shard_map/all_gather | solution.py:141
  132.8 216.6 %all-gather.16.cloned.1.call-start = ((), (), s32[]{:S(2)}) async-start(), calls=%async_computation.10 | async-start | bytes 3145728 | tf_op jit(solution)/shard_map/all_gather | solution.py:142
  133.4 387.7 %all-gather.20.cloned.1.call-start = ((), (), s32[]{:S(2)}) async-start(), calls=%async_computation.16 | async-start | bytes 10485760 | tf_op jit(solution)/shard_map/all_gather | solution.py:55
  282.0 7.6 copy-start.1
  297.8 51.6 %copy-start.56 = (f32[1024]{0:T(1024)S(1)}, f32[1024]{0:T(1024)}, u32[]{:S(2)}) copy-start(f32[1024]{0:T(1024)} %param.26) | copy-start | bytes 12292
  349.4 15.7 %copy-start.14 = (f32[1024,1024]{1,0:T(8,128)S(1)}, f32[1024,1024]{1,0:T(8,128)}, u32[]{:S(2)}) copy-start(f32[1024,1024]{1,0:T(8,128)} %fusion.85) | copy-start | bytes 12582916
  371.4 299.6 %all-gather.22.cloned.1.call-start = ((), (), s32[]{:S(2)}) async-start(), calls=%async_computation.17 | async-start | bytes 10485760 | tf_op jit(solution)/shard_map/all_gather | solution.py:55
  678.4 5.5 copy-start.4
  678.4 5.5 copy-start.7
  678.4 5.9 copy-start.11
  697.8 12.3 all-to-all-start.2
  701.3 332.9 %all-gather.24.cloned.1.call-start = ((), (), s32[]{:S(2)}) async-start(), calls=%async_computation.18 | async-start | bytes 10485760 | tf_op jit(solution)/shard_map/all_gather | solution.py:55
  874.5 4.0 copy-start.32
  882.3 4.9 copy-start.12
  887.1 179.4 %reduce-scatter.11.cloned.1.call-start = ((), (), s32[]{:S(2)}) async-start(), calls=%async_computation.14 | async-start | bytes 3145728 | tf_op jit(solution)/shard_map/reduce_scatter | solution.py:274
  892.5 6.9 copy-start.16
  892.5 208.2 %reduce-scatter.9.cloned.1.call-start = ((), (), s32[]{:S(2)}) async-start(), calls=%async_computation.13 | async-start | bytes 3145728 | tf_op jit(solution)/shard_map/reduce_scatter | solution.py:271
  899.3 230.2 %reduce-scatter.5.cloned.1.call-start = ((), (), s32[]{:S(2)}) async-start(), calls=%async_computation.11 | async-start | bytes 2359296 | tf_op jit(solution)/shard_map/reduce_scatter | solution.py:265
  904.0 243.0 %reduce-scatter.7.cloned.1.call-start = ((), (), s32[]{:S(2)}) async-start(), calls=%async_computation.12 | async-start | bytes 786432 | tf_op jit(solution)/shard_map/reduce_scatter | solution.py:268
  1034.2 7.6 copy-start.2
  1034.2 7.6 copy-start.43
  1034.2 7.6 copy-start.45
  1051.1 97.3 %copy-start.6 = (bf16[1024,1024]{1,0:T(8,128)(2,1)S(1)}, bf16[1024,1024]{1,0:T(8,128)(2,1)}, u32[]{:S(2)}) copy-start(bf16[1024,1024]{1,0:T(8,128)(2,1)} %reduce_sum.235) | copy-start | bytes 6291460
  1052.6 96.2 %copy-start.49 = (f32[1024]{0:T(1024)S(1)}, f32[1024]{0:T(1024)}, u32[]{:S(2)}) copy-start(f32[1024]{0:T(1024)} %get-tuple-element.388) | copy-start | bytes 12292
  1052.6 96.2 %copy-start.48 = (f32[1024]{0:T(1024)S(1)}, f32[1024]{0:T(1024)}, u32[]{:S(2)}) copy-start(f32[1024]{0:T(1024)} %get-tuple-element.290) | copy-start | bytes 12292
  1052.6 96.2 %copy-start.57 = (f32[1024]{0:T(1024)S(1)}, f32[1024]{0:T(1024)}, u32[]{:S(2)}) copy-start(f32[1024]{0:T(1024)} %get-tuple-element.365) | copy-start | bytes 12292
  1052.6 165.9 %all-reduce.18.cloned.1.call-start = ((), (), s32[]{:S(2)}) async-start(), calls=%async_computation.19 | async-start | bytes 6291456 | tf_op jit(solution)/shard_map/psum | solution.py:279
  1218.5 7.2 copy-start.31
  (29 other events, 72.8 us)
Sparse Core Ops, SparseCore 0:
  10.1 29.8 all-gather.11
  132.2 149.7 all-gather.17
  283.6 31.2 all-gather.13
  316.3 33.0 all-gather.15
  371.5 149.5 all-gather.19
  523.1 147.7 all-gather.21
  887.2 146.8 all-gather.23
  1036.4 30.0 reduce-scatter.10
  1068.8 31.8 reduce-scatter.8
  1103.4 26.1 reduce-scatter.4
  1132.4 14.6 reduce-scatter.6
  1149.5 68.9 all-reduce.17
